TPU v7x, 16 devices: a whole 2x2x2 slice. The times are simulated.
16 devices in a mesh: tp: 2 (over z), dp: 8 (over y, x, core).
Axes of the slice: x: 2, y: 2, z: 2, core: 2. Of those that a mesh axis runs over, the one named last changes fastest.
Arguments:
- a_mat: bfloat16 [4096, 32768], P(('dp', 'tp'))
- b_mat: bfloat16 [32768, 14336], P(('dp', 'tp'))
Outputs:
- output: bfloat16 [4096, 14336], P(('dp', 'tp'))
All inputs are finite; a program needn't handle non-finite values.
Results may differ from a plain program's by a relative error of at most 0.001.
Values are sent between devices in bfloat16 or wider.
A program may use at most 1 GiB of HBM per device.

v0:
```python
import jax
import jax.numpy as jnp
from jax import lax
from jax.sharding import PartitionSpec as P


def solution(mesh):
    spec_rows = P(("dp", "tp"), None)

    def local_block(a_rows, b_rows):
        a_cols = lax.all_to_all(a_rows, "dp", 1, 0, tiled=True)
        b_slab = lax.all_gather(b_rows, "tp", axis=0, tiled=True)
        part_prod = jnp.dot(a_cols, b_slab, preferred_element_type=jnp.float32)
        summed = lax.psum_scatter(part_prod, "dp", scatter_dimension=0, tiled=True)
        return summed.astype(jnp.bfloat16)

    return jax.shard_map(local_block, mesh=mesh, in_specs=(spec_rows, spec_rows), out_specs=spec_rows, check_vma=False)
```

profile of v0, /device:TPU:0, one launch (start us, length us, event | category | flops | bytes accessed | tf_op | source)
XLA Modules:
  0.0 2227.4 jit_solution(14535339844575910980)
XLA Ops:
  6.5 0.0 all-gather.2.cloned.1.call-start
  6.5 0.7 all-gather.2.cloned.1.call-update
  7.3 0.0 reduce-scatter.2.cloned.1.call-start
  7.3 22.4 %copy.3 = bf16[256,32768]{0,1:T(8,128)(2,1)} copy(bf16[256,32768]{1,0:T(8,128)(2,1)} %param.2) | data formatting | bytes 33554432 | tf_op args[0]
  29.7 192.1 %all_to_all.19 = bf16[256,8,4096]{0,2,1:T(8,128)(2,1)} all-to-all(bf16[256,8,4096]{0,2,1:T(8,128)(2,1)} %bitcast.6), channel_id=1, replica_groups=mesh['tp'=2,'dp'=8] {'dp'}, dimensions={1} | all-to-all | bytes 33554432 | tf_op jit(solution)/shard_map/all_to_all | solution.py:11
  221.7 20.9 copy.4
  242.6 1099.6 %all-gather.2.cloned.1.call-done = bf16[4096,14336]{1,0:T(8,128)(2,1)} async-done(((bf16[2048,14336]{1,0:T(8,128)(2,1)}), bf16[4096,14336]{1,0:T(8,128)(2,1)}) %all-gather.2.cloned.1.call-update) | async-done | bytes 117440528 | tf_op jit(solution)/shard_map/all_gather | solution.py:12
  1342.3 258.4 %fusion = f32[2048,14336]{1,0:T(8,128)} fusion(bf16[2048,4096]{1,0:T(8,128)(2,1)} %bitcast.7, bf16[4096,14336]{1,0:T(8,128)(2,1)} %all-gather.2.cloned.1.call-done), kind=kOutput, calls=%fused_computation | convolution fusion | flops 240518168576 | bytes 251658240 | tf_op jit(solution)/shard_map/dot_general | solution.py:13
  1600.7 0.0 reduce-scatter.2.cloned.1.call-update
  1600.7 610.6 %reduce-scatter.2.cloned.1.call-done = f32[256,14336]{1,0:T(8,128)} async-done(((f32[2048,14336]{1,0:T(8,128)}), f32[256,14336]{1,0:T(8,128)}) %reduce-scatter.2.cloned.1.call-update) | async-done | bytes 14680080 | tf_op jit(solution)/shard_map/reduce_scatter | solution.py:14
  2211.4 9.2 convert_element_type.3
Async XLA Ops:
  6.5 1335.7 %all-gather.2.cloned.1.call-start = ((), (), s32[]{:S(2)}) async-start(), calls=%async_computation.2 | async-start | bytes 176160768 | tf_op jit(solution)/shard_map/all_gather | solution.py:12
  7.3 2204.1 %reduce-scatter.2.cloned.1.call-start = ((), (), s32[]{:S(2)}) async-start(), calls=%async_computation.3 | async-start | bytes 132120576 | tf_op jit(solution)/shard_map/reduce_scatter | solution.py:14
Sparse Core Ops, SparseCore 0:
  8.9 1333.3 all-gather.1
  1600.8 610.4 reduce-scatter.1
where the time goes:
time: 2230 us
  waiting for transfers between devices  1710 us (77%)
  matrix products  258 us (12%)
  blocking collectives  192 us (9%)
  local copies, waits for them, and re-layouts  43.3 us (2%)
    all_gather x1, waiting for transfers between devices, local_block(): b_slab = lax.all_gather(b_rows, 'tp', axis=0, tiled=True)  1100 us
    reduce_scatter x1, waiting for transfers between devices, local_block(): summed = lax.psum_scatter(part_prod, 'dp', scatter_dimension=0, tiled=True)  611 us
    dot_general x1, matrix products, local_block(): part_prod = jnp.dot(a_cols, b_slab, preferred_element_type=jnp.float32)  258 us
    all_to_all x1, blocking collectives, local_block(): a_cols = lax.all_to_all(a_rows, 'dp', 1, 0, tiled=True)  192 us
  transfers between devices with their start and end apart: 2, of which 2 were waited for; matrix products, arithmetic and copies ran while one was open for 2% of the time, Pallas kernels for 0%

commit v1 on v0

v1 whole, which is shorter than its diff:
```python
import functools

import jax
import jax.numpy as jnp
from jax import lax
from jax.experimental import pallas as pl
from jax.experimental.pallas import tpu as pltpu
from jax.sharding import PartitionSpec as P

MESH = pl.DeviceIdType.MESH
W = 128
G = 3
LOOK = 4


def bits_of(d):
    return (d // 4, (d // 2) % 2, d % 2)


def kernel(a_hbm, b_hbm, c_hbm, bx_hbm, a_v, b_v, p_v, r1_v, s2_v, r2_v, s3_v, r3_v, o_v,
           a_send, a_recv, a_loc, bx_send, bx_recv, b_sem, s1_sem, r1_sem, s2_sem, r2_sem, s3_sem, r3_sem, o_sem, credit):
    rows = a_hbm.shape[0]
    depth, columns = b_hbm.shape
    strips = columns // W
    rem = strips % G
    tiles = (strips + G - 1) // G
    lead = (G - rem) % G

    dp, tp = lax.axis_index("dp"), lax.axis_index("tp")
    core, x, y, z = dp % 2, (dp // 2) % 2, dp // 4, tp

    def flip(v, bit):
        return v + bit - 2 * v * bit

    def device(bits, other=0):
        return {"dp": flip(y, bits[1]) * 4 + flip(x, bits[0]) * 2 + flip(core, other), "tp": flip(z, bits[2])}

    axis_nbr = [device((1, 0, 0)), device((0, 1, 0)), device((0, 0, 1))]
    partner = device((0, 0, 0), 1)

    barrier = pltpu.get_barrier_semaphore()
    for d in range(1, 8):
        pl.semaphore_signal(barrier, inc=1, device_id=device(bits_of(d)), device_id_type=MESH)
    pl.semaphore_signal(barrier, inc=1, device_id=partner, device_id_type=MESH)

    def past_first(t):
        return (t + tiles) // (tiles + 1)

    def tile_col(t):
        return pl.multiple_of((t * G - lead * past_first(t)) * W, W)

    def a_copy(d, h):
        to = device(bits_of(d), h)
        col = pl.multiple_of((to["dp"] * 2 + to["tp"]) * depth, depth)
        src = a_hbm.at[:, pl.ds(col, depth)]
        dst = a_v.at[d, :, pl.ds(h * depth, depth)]
        if d == 0:
            return pltpu.make_async_copy(src, dst, a_loc.at[h])
        return pltpu.make_async_remote_copy(
            src_ref=src, dst_ref=dst, send_sem=a_send.at[d, h], recv_sem=a_recv.at[d, h],
            device_id=device(bits_of(d)), device_id_type=MESH)

    def bx_copy(t):
        cols = pl.ds(tile_col(t), G * W)
        return pltpu.make_async_remote_copy(
            src_ref=b_hbm.at[:, cols], dst_ref=bx_hbm.at[t], send_sem=bx_send.at[t], recv_sem=bx_recv.at[t],
            device_id=partner, device_id_type=MESH)

    def b_copies(t):
        slot = t % 2
        cols = pl.ds(tile_col(t), G * W)
        return (pltpu.make_async_copy(b_hbm.at[:, cols], b_v.at[slot, pl.ds(0, depth), :], b_sem.at[slot, 0]),
                pltpu.make_async_copy(bx_hbm.at[t], b_v.at[slot, pl.ds(depth, depth), :], b_sem.at[slot, 1]))

    def b_fetch(t):
        bx_copy(t).wait_recv()
        for copy in b_copies(t):
            copy.start()

    for copy in (a_copy(0, 0), a_copy(0, 1)):
        copy.start()
    pl.semaphore_wait(barrier, 8)
    bx_copy(0).start()

    groups = ((7,), (6, 1), (5, 2), (3, 4))
    halves = [[a_copy(d, h) for d in group] for group in groups for h in range(2)]
    for i, half in enumerate(halves):
        if i >= 2:
            for copy in halves[i - 2]:
                copy.wait_recv()
        for copy in half:
            copy.start()
        if i == 1:
            for t in range(1, min(LOOK, tiles)):
                bx_copy(t).start()
            b_fetch(0)
    for copy in (a_copy(0, 0), a_copy(0, 1)):
        copy.wait()
    for half in halves[-2:]:
        for copy in half:
            copy.wait_recv()

    def send(src, dst, send_sem, recv_sem, axis):
        return pltpu.make_async_remote_copy(
            src_ref=src, dst_ref=dst, send_sem=send_sem, recv_sem=recv_sem, device_id=axis_nbr[axis], device_id_type=MESH)

    def send1(t, g):
        s = t % 2
        return send(p_v.at[s, g, 1], r1_v.at[s, g], s1_sem.at[s, g], r1_sem.at[s, g], g)

    def send2(t, g):
        s = t % 2
        return send(s2_v.at[s, g, pl.ds(2, 2)], r2_v.at[s, g], s2_sem.at[s, g], r2_sem.at[s, g], (g + 1) % 3)

    def send3(t, g):
        s = t % 2
        return send(s3_v.at[s, g, 1], r3_v.at[s, g], s3_sem.at[s, g], r3_sem.at[s, g], (g + 2) % 3)

    def out_copy(t, g):
        s = t % 2
        col = tile_col(t) + g * W
        return pltpu.make_async_copy(o_v.at[s, g], c_hbm.at[:, pl.ds(pl.multiple_of(col, W), W)], o_sem.at[s, g])

    def first(g):
        return 0 if rem == 0 or g < rem else 1

    def when(t, low, high, fn):
        pl.when(jnp.logical_and(t >= low, t < high))(fn)

    def start_with_credit(t, g, phase, copy):
        when(t, first(g) + 2, tiles, lambda: pl.semaphore_wait(credit.at[phase, g], 1))
        when(t, first(g), tiles, lambda: copy(t, g).start())

    def give_credit(t, g, phase):
        when(t, first(g), tiles - 2, lambda: pl.semaphore_signal(
            credit.at[phase, g], inc=1, device_id=axis_nbr[(g + phase) % 3], device_id_type=MESH))

    def free(t, g, copy):
        when(t, first(g) + 2, tiles + 2, lambda: copy(t - 2, g).wait_send())

    def partials(t):
        s = t % 2

        def body(d, carry):
            b = bits_of(d)
            part = jnp.dot(a_v[d], b_v[s], preferred_element_type=jnp.float32)
            for g in range(G):
                p_v[s, g, b[g], b[(g + 1) % 3] * 2 + b[(g + 2) % 3]] = part[:, g * W:(g + 1) * W]
            return carry

        lax.fori_loop(0, 8, body, 0)

    def step(i, carry):
        t = i
        when(t, 0, tiles - LOOK, lambda: bx_copy(t + LOOK).start())
        when(t, 0, tiles - 1, lambda: b_fetch(t + 1))
        for g in range(G):
            free(t, g, send1)

        def products():
            for copy in b_copies(t):
                copy.wait()
            partials(t)

        when(t, 0, tiles, products)
        for g in range(G):
            start_with_credit(t, g, 0, send1)

        t1 = i - 1
        for g in range(G):
            free(t1, g, send2)

            def add1(g=g):
                s = t1 % 2
                send1(t1, g).wait_recv()
                s2_v[s, g] = p_v[s, g, 0] + r1_v[s, g]

            when(t1, first(g), tiles, add1)
            give_credit(t1, g, 0)
            start_with_credit(t1, g, 1, send2)

        t2 = i - 2
        for g in range(G):
            free(t2, g, send3)

            def add2(g=g):
                s = t2 % 2
                send2(t2, g).wait_recv()
                s3_v[s, g] = s2_v[s, g, 0:2] + r2_v[s, g]

            when(t2, first(g), tiles, add2)
            give_credit(t2, g, 1)
            start_with_credit(t2, g, 2, send3)

        t3 = i - 3
        for g in range(G):
            when(t3, first(g) + 2, tiles + 2, lambda g=g: out_copy(t3 - 2, g).wait())

            def add3(g=g):
                s = t3 % 2
                send3(t3, g).wait_recv()
                o_v[s, g] = (s3_v[s, g, 0] + r3_v[s, g]).astype(jnp.bfloat16)
                out_copy(t3, g).start()

            when(t3, first(g), tiles, add3)
            give_credit(t3, g, 2)
        return carry

    lax.fori_loop(0, tiles + 5, step, 0)

    for half in halves:
        for copy in half:
            copy.wait_send()

    def drain(t, carry):
        bx_copy(t).wait_send()
        return carry

    lax.fori_loop(0, tiles, drain, 0)


def solution(mesh):
    spec_rows = P(("dp", "tp"), None)

    def local_block(a_rows, b_rows):
        rows, inner = a_rows.shape
        depth, columns = b_rows.shape
        tiles = -(-columns // (G * W))
        f32, bf16 = jnp.float32, jnp.bfloat16
        dma = pltpu.SemaphoreType.DMA
        out = pl.pallas_call(
            kernel,
            name="matmul_reduce_scatter",
            out_shape=(jax.ShapeDtypeStruct((rows, columns), bf16), jax.ShapeDtypeStruct((tiles, depth, G * W), bf16)),
            in_specs=[pl.BlockSpec(memory_space=pl.ANY)] * 2,
            out_specs=(pl.BlockSpec(memory_space=pl.ANY),) * 2,
            scratch_shapes=[
                pltpu.VMEM((8, rows, 2 * depth), bf16),
                pltpu.VMEM((2, 2 * depth, G * W), bf16),
                pltpu.VMEM((2, G, 2, 4, rows, W), f32),
                pltpu.VMEM((2, G, 4, rows, W), f32),
                pltpu.VMEM((2, G, 4, rows, W), f32),
                pltpu.VMEM((2, G, 2, rows, W), f32),
                pltpu.VMEM((2, G, 2, rows, W), f32),
                pltpu.VMEM((2, G, rows, W), f32),
                pltpu.VMEM((2, G, rows, W), bf16),
                dma((8, 2)), dma((8, 2)), dma((2,)),
                dma((tiles,)), dma((tiles,)), dma((2, 2)),
                dma((2, G)), dma((2, G)), dma((2, G)), dma((2, G)), dma((2, G)), dma((2, G)), dma((2, G)),
                pltpu.SemaphoreType.REGULAR((3, G)),
            ],
            compiler_params=pltpu.CompilerParams(
                collective_id=0, has_side_effects=True, vmem_limit_bytes=60 * 1024 * 1024),
            cost_estimate=pl.CostEstimate(
                flops=2 * 8 * rows * 2 * depth * columns, bytes_accessed=6 * depth * columns, transcendentals=0),
        )(a_rows, b_rows)
        return out[0]

    return jax.shard_map(local_block, mesh=mesh, in_specs=(spec_rows, spec_rows), out_specs=spec_rows, check_vma=False)
```

time: 2230 us -> 993 us (0.45)
  waiting for transfers between devices: 1710 us -> 0 us
  Pallas kernels: 0 us -> 982 us
  matrix products: 258 us -> 0 us
  blocking collectives: 192 us -> 0 us
  local copies, waits for them, and re-layouts: 43.3 us -> 6.9 us
    all_gather x1 -> x0, waiting for transfers between devices: 1100 us -> none  [local_block(): b_slab = lax.all_gather(b_rows, 'tp', axis=0, tiled=True)]
    pallas_call x0 -> x1, Pallas kernels: none -> 982 us  [local_block(): pl.pallas_call(kernel, name='matmul_reduce_scatter', out_shape=(jax.Shape...]
    reduce_scatter x1 -> x0, waiting for transfers between devices: 611 us -> none  [local_block(): summed = lax.psum_scatter(part_prod, 'dp', scatter_dimension=0, tiled=True)]
    dot_general x1 -> x0, matrix products: 258 us -> none  [local_block(): part_prod = jnp.dot(a_cols, b_slab, preferred_element_type=jnp.float32)]
    all_to_all x1 -> x0, blocking collectives: 192 us -> none  [local_block(): a_cols = lax.all_to_all(a_rows, 'dp', 1, 0, tiled=True)]
  transfers between devices with their start and end apart: 2 -> 0, of which waited for: 2 -> 0; matrix products, arithmetic and copies ran while one was open for 2% -> 0% of each run, Pallas kernels for 0% -> 0%
where the time goes in v1:
time: 993 us; the launch traced here: 989 us
  Pallas kernels  982 us (99%)
    pallas_call x1, Pallas kernels, local_block(): pl.pallas_call(kernel, name='matmul_reduce_scatter', out_shape=(jax.Shape...  982 us

profile of v1, /device:TPU:0, one launch (start us, length us, event | category | flops | bytes accessed | tf_op | source)
XLA Modules:
  0.0 988.7 jit_solution(13513487442343933534)
XLA Ops:
  0.0 981.8 %matmul_reduce_scatter.1 = (bf16[256,14336]{1,0:T(8,128)(2,1)}, bf16[38,2048,384]{2,1,0:T(8,128)(2,1)}) custom-call(bf16[256,32768]{1,0:T(8,128)(2,1)} %a_hbm.1, bf16[2048,14336]{1,0:T(8,128)(2,1)} %b_hbm.1), custom_call_target="tpu_custom_call" | custom-call | flops 240518168576 | bytes 176160768 | tf_op jit(solution)/shard_map/matmul_reduce_scatter/pallas_call | solution.py:231
  981.8 6.9 copy.4

commit v2 on v1

--- a/solution.py
+++ b/solution.py
@@ -17,7 +17,7 @@
     return (d // 4, (d // 2) % 2, d % 2)
 
 
-def kernel(a_hbm, b_hbm, c_hbm, bx_hbm, a_v, b_v, p_v, r1_v, s2_v, r2_v, s3_v, r3_v, o_v,
+def kernel(a_hbm, b_hbm, c_hbm, bx_hbm, a_v, relay, b_v, p_v, r1_v, s2_v, r2_v, s3_v, r3_v, o_v,
            a_send, a_recv, a_loc, bx_send, bx_recv, b_sem, s1_sem, r1_sem, s2_sem, r2_sem, s3_sem, r3_sem, o_sem, credit):
     rows = a_hbm.shape[0]
     depth, columns = b_hbm.shape
@@ -39,9 +39,8 @@
     partner = device((0, 0, 0), 1)
 
     barrier = pltpu.get_barrier_semaphore()
-    for d in range(1, 8):
-        pl.semaphore_signal(barrier, inc=1, device_id=device(bits_of(d)), device_id_type=MESH)
-    pl.semaphore_signal(barrier, inc=1, device_id=partner, device_id_type=MESH)
+    for nbr in (*axis_nbr, partner):
+        pl.semaphore_signal(barrier, inc=1, device_id=nbr, device_id_type=MESH)
 
     def past_first(t):
         return (t + tiles) // (tiles + 1)
@@ -49,16 +48,35 @@
     def tile_col(t):
         return pl.multiple_of((t * G - lead * past_first(t)) * W, W)
 
-    def a_copy(d, h):
+    def a_cols(d, h):
         to = device(bits_of(d), h)
-        col = pl.multiple_of((to["dp"] * 2 + to["tp"]) * depth, depth)
-        src = a_hbm.at[:, pl.ds(col, depth)]
-        dst = a_v.at[d, :, pl.ds(h * depth, depth)]
-        if d == 0:
-            return pltpu.make_async_copy(src, dst, a_loc.at[h])
+        return a_hbm.at[:, pl.ds(pl.multiple_of((to["dp"] * 2 + to["tp"]) * depth, depth), depth)]
+
+    def block(ref, i, h):
+        return ref.at[i, :, pl.ds(h * depth, depth)]
+
+    def hop(n, h, src, dst, axis):
         return pltpu.make_async_remote_copy(
-            src_ref=src, dst_ref=dst, send_sem=a_send.at[d, h], recv_sem=a_recv.at[d, h],
-            device_id=device(bits_of(d)), device_id_type=MESH)
+            src_ref=src, dst_ref=dst, send_sem=a_send.at[n, h], recv_sem=a_recv.at[n, h],
+            device_id=axis_nbr[axis], device_id_type=MESH)
+
+    def hops(h):
+        return (
+            (hop(0, h, a_cols(7, h), block(relay, 0, h), 0),
+             hop(1, h, a_cols(6, h), block(relay, 1, h), 1),
+             hop(2, h, a_cols(5, h), block(relay, 2, h), 2)),
+            (hop(3, h, block(relay, 1, h), block(a_v, 6, h), 0),
+             hop(4, h, block(relay, 0, h), block(relay, 3, h), 1),
+             hop(5, h, a_cols(3, h), block(relay, 4, h), 2)),
+            (hop(6, h, block(relay, 2, h), block(a_v, 5, h), 0),
+             hop(7, h, block(relay, 4, h), block(a_v, 3, h), 1),
+             hop(8, h, block(relay, 3, h), block(a_v, 7, h), 2)),
+            (hop(9, h, a_cols(4, h), block(a_v, 4, h), 0),
+             hop(10, h, a_cols(2, h), block(a_v, 2, h), 1),
+             hop(11, h, a_cols(1, h), block(a_v, 1, h), 2)))
+
+    def a_own(h):
+        return pltpu.make_async_copy(a_cols(0, h), block(a_v, 0, h), a_loc.at[h])
 
     def bx_copy(t):
         cols = pl.ds(tile_col(t), G * W)
@@ -77,29 +95,6 @@
         for copy in b_copies(t):
             copy.start()
 
-    for copy in (a_copy(0, 0), a_copy(0, 1)):
-        copy.start()
-    pl.semaphore_wait(barrier, 8)
-    bx_copy(0).start()
-
-    groups = ((7,), (6, 1), (5, 2), (3, 4))
-    halves = [[a_copy(d, h) for d in group] for group in groups for h in range(2)]
-    for i, half in enumerate(halves):
-        if i >= 2:
-            for copy in halves[i - 2]:
-                copy.wait_recv()
-        for copy in half:
-            copy.start()
-        if i == 1:
-            for t in range(1, min(LOOK, tiles)):
-                bx_copy(t).start()
-            b_fetch(0)
-    for copy in (a_copy(0, 0), a_copy(0, 1)):
-        copy.wait()
-    for half in halves[-2:]:
-        for copy in half:
-            copy.wait_recv()
-
     def send(src, dst, send_sem, recv_sem, axis):
         return pltpu.make_async_remote_copy(
             src_ref=src, dst_ref=dst, send_sem=send_sem, recv_sem=recv_sem, device_id=axis_nbr[axis], device_id_type=MESH)
@@ -138,22 +133,73 @@
     def free(t, g, copy):
         when(t, first(g) + 2, tiles + 2, lambda: copy(t - 2, g).wait_send())
 
+    def partial(t, d):
+        s = t % 2
+        b = bits_of(d)
+        part = jnp.dot(a_v[d], b_v[s], preferred_element_type=jnp.float32)
+        for g in range(G):
+            p_v[s, g, b[g], b[(g + 1) % 3] * 2 + b[(g + 2) % 3]] = part[:, g * W:(g + 1) * W]
+
     def partials(t):
-        s = t % 2
-
         def body(d, carry):
-            b = bits_of(d)
-            part = jnp.dot(a_v[d], b_v[s], preferred_element_type=jnp.float32)
-            for g in range(G):
-                p_v[s, g, b[g], b[(g + 1) % 3] * 2 + b[(g + 2) % 3]] = part[:, g * W:(g + 1) * W]
+            partial(t, d)
             return carry
 
         lax.fori_loop(0, 8, body, 0)
+
+    slots = [hops(0), hops(1)]
+    for h in range(2):
+        a_own(h).start()
+    pl.semaphore_wait(barrier, 4)
+    bx_copy(0).start()
+    for h in range(2):
+        for copy in slots[h][0]:
+            copy.start()
+    for t in range(1, min(LOOK, tiles)):
+        bx_copy(t).start()
+    for t in range(2):
+        b_fetch(t)
+    for h in range(2):
+        slots[h][0][0].wait_recv()
+        slots[h][0][1].wait_recv()
+        for copy in slots[h][1]:
+            copy.start()
+    for t in range(2):
+        for copy in b_copies(t):
+            copy.wait()
+    for h in range(2):
+        a_own(h).wait()
+    partial(0, 0)
+    partial(1, 0)
+    for h in range(2):
+        slots[h][0][2].wait_recv()
+        slots[h][1][1].wait_recv()
+        slots[h][1][2].wait_recv()
+        for copy in slots[h][2]:
+            copy.start()
+    for h in range(2):
+        for copy in slots[h][3]:
+            copy.start()
+    for h in range(2):
+        slots[h][1][0].wait_recv()
+    partial(0, 6)
+    partial(1, 6)
+    for h in range(2):
+        for copy in slots[h][2]:
+            copy.wait_recv()
+    for t in range(2):
+        for d in (3, 5, 7):
+            partial(t, d)
+    for h in range(2):
+        for copy in slots[h][3]:
+            copy.wait_recv()
+    for d in (1, 2, 4):
+        partial(0, d)
 
     def step(i, carry):
         t = i
         when(t, 0, tiles - LOOK, lambda: bx_copy(t + LOOK).start())
-        when(t, 0, tiles - 1, lambda: b_fetch(t + 1))
+        when(t, 1, tiles - 1, lambda: b_fetch(t + 1))
         for g in range(G):
             free(t, g, send1)
 
@@ -162,7 +208,13 @@
                 copy.wait()
             partials(t)
 
-        when(t, 0, tiles, products)
+        when(t, 2, tiles, products)
+
+        def rest():
+            for d in (1, 2, 4):
+                partial(1, d)
+
+        when(t, 1, 2, rest)
         for g in range(G):
             start_with_credit(t, g, 0, send1)
 
@@ -208,9 +260,10 @@
 
     lax.fori_loop(0, tiles + 5, step, 0)
 
-    for half in halves:
-        for copy in half:
-            copy.wait_send()
+    for h in range(2):
+        for slot in slots[h]:
+            for copy in slot:
+                copy.wait_send()
 
     def drain(t, carry):
         bx_copy(t).wait_send()
@@ -236,6 +289,7 @@
             out_specs=(pl.BlockSpec(memory_space=pl.ANY),) * 2,
             scratch_shapes=[
                 pltpu.VMEM((8, rows, 2 * depth), bf16),
+                pltpu.VMEM((5, rows, 2 * depth), bf16),
                 pltpu.VMEM((2, 2 * depth, G * W), bf16),
                 pltpu.VMEM((2, G, 2, 4, rows, W), f32),
                 pltpu.VMEM((2, G, 4, rows, W), f32),
@@ -244,7 +298,7 @@
                 pltpu.VMEM((2, G, 2, rows, W), f32),
                 pltpu.VMEM((2, G, rows, W), f32),
                 pltpu.VMEM((2, G, rows, W), bf16),
-                dma((8, 2)), dma((8, 2)), dma((2,)),
+                dma((12, 2)), dma((12, 2)), dma((2,)),
                 dma((tiles,)), dma((tiles,)), dma((2, 2)),
                 dma((2, G)), dma((2, G)), dma((2, G)), dma((2, G)), dma((2, G)), dma((2, G)), dma((2, G)),
                 pltpu.SemaphoreType.REGULAR((3, G)),

time: 993 us -> 942 us (0.949)
  Pallas kernels: 982 us -> 935 us
    pallas_call x1, Pallas kernels: 982 us -> 935 us  [local_block(): pl.pallas_call(kernel, name='matmul_reduce_scatter', out_shape=(jax.Shape...]
where the time goes in v2:
time: 942 us
  Pallas kernels  935 us (99%)
    pallas_call x1, Pallas kernels, local_block(): pl.pallas_call(kernel, name='matmul_reduce_scatter', out_shape=(jax.Shape...  935 us

profile of v2, /device:TPU:0, one launch (start us, length us, event | category | flops | bytes accessed | tf_op | source)
XLA Modules:
  0.0 941.8 jit_solution(16728489524073880161)
XLA Ops:
  0.0 934.9 %matmul_reduce_scatter.1 = (bf16[256,14336]{1,0:T(8,128)(2,1)}, bf16[38,2048,384]{2,1,0:T(8,128)(2,1)}) custom-call(bf16[256,32768]{1,0:T(8,128)(2,1)} %a_hbm.1, bf16[2048,14336]{1,0:T(8,128)(2,1)} %b_hbm.1), custom_call_target="tpu_custom_call" | custom-call | flops 240518168576 | bytes 176160768 | tf_op jit(solution)/shard_map/matmul_reduce_scatter/pallas_call | solution.py:284
  934.9 6.9 copy.4

commit v3 on v0

v3 whole, which is shorter than its diff:
```python
import jax
import jax.numpy as jnp
from jax import lax
from jax.experimental import pallas as pl
from jax.experimental.pallas import tpu as pltpu
from jax.sharding import PartitionSpec as P

MESH = pl.DeviceIdType.MESH
W = 128
C = 2 * W
LOOK = 4
D3 = 6
DO = 6
AX, AY, AZ = 0, 1, 2


def bits_of(d):
    return (d // 4, (d // 2) % 2, d % 2)


def counts(columns):
    paired = columns // C // 4
    return columns // C - 2 * paired, paired


def kernel(a_hbm, b_hbm, c_hbm, bx_hbm, bz_hbm, bxz_hbm, relay,
           a_v, b_v, p_v, r1_v, s2_v, r2_v, s3_v, r3_v, o_v, q_v,
           hop_send, hop_recv, own_sem, bx_send, bx_recv, bxz_send, bxz_recv, ch_send, ch_recv, b_sem,
           s1_sem, r1_sem, s2_sem, r2_sem, s3_sem, r3_sem, o_sem, ql_sem, qs_sem, qr_sem, credit):
    depth, columns = b_hbm.shape
    plain, paired = counts(columns)
    tiles = plain + paired
    half = depth // 2
    chunks = 16 + 2 * paired
    rate = max(120, -(-1800 // plain), -(-100 * (16 + 2 * paired) // (tiles - 1)))

    dp, tp = lax.axis_index("dp"), lax.axis_index("tp")
    core, x, y, z = dp % 2, (dp // 2) % 2, dp // 4, tp

    def flip(v, bit):
        return v + bit - 2 * v * bit

    def device(bits, other=0):
        return {"dp": flip(y, bits[1]) * 4 + flip(x, bits[0]) * 2 + flip(core, other), "tp": flip(z, bits[2])}

    axis_nbr = [device((1, 0, 0)), device((0, 1, 0)), device((0, 0, 1))]
    partner = device((0, 0, 0), 1)

    barrier = pltpu.get_barrier_semaphore()
    for nbr in (*axis_nbr, partner):
        pl.semaphore_signal(barrier, inc=1, device_id=nbr, device_id_type=MESH)

    def send(src, dst, send_sem, recv_sem, to):
        return pltpu.make_async_remote_copy(
            src_ref=src, dst_ref=dst, send_sem=send_sem, recv_sem=recv_sem, device_id=to, device_id_type=MESH)

    def when(t, low, high, fn):
        pl.when(jnp.logical_and(t >= low, t < high))(fn)

    def is_paired(t):
        return (t + tiles - plain) // tiles

    def tile_cols(t, g=None):
        col = t * C + is_paired(t) * ((t - plain) * C + z * C)
        if g is None:
            return pl.ds(pl.multiple_of(col, W), C)
        return pl.ds(pl.multiple_of(col + g * W, W), W)

    def their_cols(q):
        return pl.ds(pl.multiple_of((plain + 2 * q + 1 - z) * C, W), C)

    def a_cols(bits, h):
        to = device(bits, h)
        return a_hbm.at[:, pl.ds(pl.multiple_of((to["dp"] * 2 + to["tp"]) * depth, depth), depth)]

    def near(d, h):
        return a_v.at[d, :, pl.ds(h * depth, depth)]

    def far(d, h):
        return a_v.at[d, :, pl.ds((2 + h) * depth, depth)]

    def held(i, h):
        return relay.at[i, :, pl.ds(h * depth, depth)]

    def hop(n, h, src, dst, axis):
        return send(src, dst, hop_send.at[n, h], hop_recv.at[n, h], axis_nbr[axis])

    both = range(2)
    x_far = [hop(0, h, a_cols((1, 0, 1), h), far(4, h), AX) for h in both]
    y_far = [hop(1, h, a_cols((0, 1, 1), h), far(2, h), AY) for h in both]
    z_own = [hop(2, h, a_cols((0, 0, 1), h), near(1, h), AZ) for h in both]
    xy_far1 = [hop(3, h, a_cols((1, 1, 1), h), held(0, h), AX) for h in both]
    yx_near1 = [hop(4, h, a_cols((1, 1, 0), h), held(1, h), AY) for h in both]
    z_x = [hop(5, h, far(4, h), near(5, h), AZ) for h in both]
    z_y = [hop(6, h, far(2, h), near(3, h), AZ) for h in both]
    yx_near2 = [hop(7, h, held(1, h), near(6, h), AX) for h in both]
    xy_far2 = [hop(8, h, held(0, h), far(6, h), AY) for h in both]
    x_near = [hop(9, h, a_cols((1, 0, 0), h), near(4, h), AX) for h in both]
    y_near = [hop(10, h, a_cols((0, 1, 0), h), near(2, h), AY) for h in both]
    z_xy = [hop(11, h, far(6, h), near(7, h), AZ) for h in both]
    all_hops = (x_far, y_far, z_own, xy_far1, yx_near1, z_x, z_y, yx_near2, xy_far2, x_near, y_near, z_xy)
    own = [pltpu.make_async_copy(a_cols((0, 0, 0), h), near(0, h), own_sem.at[h]) for h in both]
    own += [pltpu.make_async_copy(a_cols((0, 0, 1), h), far(0, h), own_sem.at[2 + h]) for h in both]

    def a_chunk(n):
        d, k = (n // 4) * 2, n % 4
        return send(a_v.at[d, :, pl.ds(pl.multiple_of(k * half, half), half)],
                    a_v.at[d + 1, :, pl.ds(pl.multiple_of(2 * depth + k * half, half), half)],
                    ch_send.at[n], ch_recv.at[n], axis_nbr[AZ])

    def b_chunk(q, h):
        rows = pl.ds(pl.multiple_of(h * half, half), half)
        n = 16 + 2 * q + h
        return send(b_hbm.at[rows, their_cols(q)], bz_hbm.at[q, rows], ch_send.at[n], ch_recv.at[n], axis_nbr[AZ])

    def start_chunks(i):
        def body(n, carry):
            when(n, 0, 16, lambda: a_chunk(n).start())
            when(n, 16, chunks, lambda: b_chunk((n - 16) // 2, (n - 16) % 2).start())
            return carry

        lax.fori_loop(rate * i // 100, rate * (i + 1) // 100, body, 0)

    def bx_copy(t):
        return send(b_hbm.at[:, tile_cols(t)], bx_hbm.at[t], bx_send.at[t], bx_recv.at[t], partner)

    def bxz_copy(q):
        return send(bz_hbm.at[q], bxz_hbm.at[q], bxz_send.at[q], bxz_recv.at[q], partner)

    def b_piece(t, k):
        src = (b_hbm.at[:, tile_cols(t)], bx_hbm.at[t], bz_hbm.at[t - plain], bxz_hbm.at[t - plain])[k]
        return pltpu.make_async_copy(src, b_v.at[t % 2, pl.ds(k * depth, depth)], b_sem.at[t % 2, k])

    def fetch_near(t):
        b_piece(t, 0).start()
        bx_copy(t).wait_recv()
        b_piece(t, 1).start()

    def fetch_far(t):
        for h in both:
            b_chunk(t - plain, h).wait_recv()
        bxz_copy(t - plain).start()
        b_piece(t, 2).start()

    def fetch_last(t):
        bxz_copy(t - plain).wait_recv()
        b_piece(t, 3).start()

    def partial(t, d, k):
        s = t % 2
        dx, dy, dz = bits_of(d)
        part = jnp.dot(a_v[d, :, 0:k * depth], b_v[s, 0:k * depth], preferred_element_type=jnp.float32)
        p_v[s, 0, dx, dy * 2 + dz] = part[:, 0:W]
        p_v[s, 1, dy, dx * 2 + dz] = part[:, W:C]

    def partials(t, k, n=8, order=lambda j: j):
        def body(j, carry):
            partial(t, order(j), k)
            return carry

        lax.fori_loop(0, n, body, 0)

    def first_two(n, order):
        def body(j, carry):
            partial(j // n, order(j % n), 2)
            return carry

        lax.fori_loop(0, 2 * n, body, 0)

    def send1(t, g):
        s = t % 2
        return send(p_v.at[s, g, 1], r1_v.at[s, g], s1_sem.at[s, g], r1_sem.at[s, g], axis_nbr[g])

    def send2(t, g):
        s = t % 2
        return send(s2_v.at[s, g, pl.ds(2, 2)], r2_v.at[s, g], s2_sem.at[s, g], r2_sem.at[s, g], axis_nbr[1 - g])

    def send3(t, g):
        s = t % D3
        return send(s3_v.at[s, g, 1], r3_v.at[s, g], s3_sem.at[s, g], r3_sem.at[s, g], axis_nbr[AZ])

    def out_copy(t, g):
        return pltpu.make_async_copy(o_v.at[t % 2, g], c_hbm.at[:, tile_cols(t, g)], o_sem.at[t % 2, g])

    def pair_here(t, g):
        s = t % DO
        return pltpu.make_async_copy(q_v.at[s, g, 0], c_hbm.at[:, tile_cols(t, g)], ql_sem.at[s, g])

    def pair_there(t, g):
        s = t % DO
        return send(q_v.at[s, g, 1], c_hbm.at[:, tile_cols(t, g)], qs_sem.at[s, g], qr_sem.at[t - plain, g], axis_nbr[AZ])

    def take(t, g, phase, slots, high):
        when(t, slots, high, lambda: pl.semaphore_wait(credit.at[phase, g], 1))

    def give(t, g, phase, axis, slots, high):
        when(t, 0, high - slots, lambda: pl.semaphore_signal(
            credit.at[phase, g], inc=1, device_id=axis_nbr[axis], device_id_type=MESH))

    for copy in own:
        copy.start()
    pl.semaphore_wait(barrier, 4)
    bx_copy(0).start()
    bx_copy(1).start()
    for group in (x_far, y_far, z_own):
        for copy in group:
            copy.start()
    for group in (xy_far1, yx_near1):
        for copy in group:
            copy.start()
    for t in range(2, min(LOOK, tiles)):
        bx_copy(t).start()
    for t in range(2):
        fetch_near(t)
    for h in both:
        x_far[h].wait_recv()
        z_x[h].start()
    for h in both:
        y_far[h].wait_recv()
        z_y[h].start()
    for h in both:
        yx_near1[h].wait_recv()
        yx_near2[h].start()
        xy_far1[h].wait_recv()
        xy_far2[h].start()
    for copy in x_near + y_near:
        copy.start()
    for t in range(2):
        for k in range(2):
            b_piece(t, k).wait()
    for copy in own:
        copy.wait()
    for copy in z_own + z_x:
        copy.wait_recv()
    first_two(3, lambda j: (3 * j * j - j) // 2)
    for h in both:
        xy_far2[h].wait_recv()
        z_xy[h].start()
    for copy in z_y + yx_near2:
        copy.wait_recv()
    first_two(2, lambda j: 3 + 3 * j)
    for copy in x_near + y_near + z_xy:
        copy.wait_recv()

    def last_three(j):
        return 2 + 2 * j + j // 2

    def step(i, carry):
        t = i
        when(t, 0, tiles, lambda: start_chunks(t))
        when(t, 0, tiles - LOOK, lambda: bx_copy(t + LOOK).start())
        when(t, 1, tiles - 1, lambda: fetch_near(t + 1))
        for g in both:
            when(t, 2, tiles + 2, lambda g=g: send1(t - 2, g).wait_send())

        def wait_b(pieces):
            for k in range(pieces):
                b_piece(t, k).wait()

        def near_products():
            wait_b(2)
            partials(t, 2)

        def all_products():
            wait_b(4)
            partials(t, 4)

        def wait_far():
            def body(n, carry):
                a_chunk(n).wait_recv()
                return carry

            lax.fori_loop(0, 16, body, 0)

        when(t, 0, 2, lambda: partials(t, 2, 3, last_three))
        when(t, 2, plain, near_products)
        when(t, plain, plain + 1, wait_far)
        when(t, plain, tiles, all_products)
        for g in both:
            take(t, g, 0, 2, tiles)
            when(t, 0, tiles, lambda g=g: send1(t, g).start())
        when(t, plain - 1, tiles - 1, lambda: fetch_far(t + 1))

        t1 = i - 1
        for g in both:
            when(t1, 2, tiles + 2, lambda g=g: send2(t1 - 2, g).wait_send())

            def add1(g=g):
                s = t1 % 2
                send1(t1, g).wait_recv()
                s2_v[s, g] = p_v[s, g, 0] + r1_v[s, g]

            when(t1, 0, tiles, add1)
            give(t1, g, 0, g, 2, tiles)
            take(t1, g, 1, 2, tiles)
            when(t1, 0, tiles, lambda g=g: send2(t1, g).start())

        t2 = i - 2
        for g in both:
            when(t2, D3, plain + D3, lambda g=g: send3(t2 - D3, g).wait_send())

            def add2(g=g):
                send2(t2, g).wait_recv()
                s3_v[t2 % D3, g] = s2_v[t2 % 2, g, 0:2] + r2_v[t2 % 2, g]

            def add2_paired(g=g):
                send2(t2, g).wait_recv()
                q_v[t2 % DO, g] = (s2_v[t2 % 2, g, 0:2] + r2_v[t2 % 2, g]).astype(jnp.bfloat16)

            def free_pair(g=g):
                pair_here(t2 - DO, g).wait()
                pair_there(t2 - DO, g).wait_send()

            def start_pair(g=g):
                pair_here(t2, g).start()
                pair_there(t2, g).start()

            when(t2, 0, plain, add2)
            when(t2, plain + DO, tiles, free_pair)
            when(t2, plain, tiles, add2_paired)
            give(t2, g, 1, 1 - g, 2, tiles)
            take(t2, g, 2, D3, plain)
            when(t2, 0, plain, lambda g=g: send3(t2, g).start())
            when(t2, plain, tiles, start_pair)

        t3 = i - 1 - D3
        for g in both:
            when(t3, 2, plain + 2, lambda g=g: out_copy(t3 - 2, g).wait())

            def add3(g=g):
                send3(t3, g).wait_recv()
                o_v[t3 % 2, g] = (s3_v[t3 % D3, g, 0] + r3_v[t3 % D3, g]).astype(jnp.bfloat16)
                out_copy(t3, g).start()

            when(t3, 0, plain, add3)
            give(t3, g, 2, AZ, D3, plain)
        when(t, plain - 1, tiles - 1, lambda: fetch_last(t + 1))
        return carry

    lax.fori_loop(0, max(tiles + 3, plain + D3 + 3), step, 0)

    for group in all_hops:
        for copy in group:
            copy.wait_send()

    def each(low, high, fn):
        def body(n, carry):
            fn(n)
            return carry

        lax.fori_loop(low, high, body, 0)

    each(0, tiles, lambda t: bx_copy(t).wait_send())
    each(0, paired, lambda q: bxz_copy(q).wait_send())
    each(0, 16, lambda n: a_chunk(n).wait_send())
    each(0, 2 * paired, lambda n: b_chunk(n // 2, n % 2).wait_send())
    for g in both:
        each(max(plain, tiles - DO), tiles, lambda t: pair_here(t, g).wait())
        each(max(plain, tiles - DO), tiles, lambda t: pair_there(t, g).wait_send())
        each(plain, tiles, lambda t: pair_there(t, g).wait_recv())


def solution(mesh):
    spec_rows = P(("dp", "tp"), None)

    def local_block(a_rows, b_rows):
        rows, inner = a_rows.shape
        depth, columns = b_rows.shape
        plain, paired = counts(columns)
        tiles = plain + paired
        f32, bf16 = jnp.float32, jnp.bfloat16
        dma = pltpu.SemaphoreType.DMA
        out = pl.pallas_call(
            kernel,
            name="matmul_reduce_scatter",
            out_shape=(
                jax.ShapeDtypeStruct((rows, columns), bf16),
                jax.ShapeDtypeStruct((tiles, depth, C), bf16),
                jax.ShapeDtypeStruct((paired, depth, C), bf16),
                jax.ShapeDtypeStruct((paired, depth, C), bf16),
                jax.ShapeDtypeStruct((2, rows, 2 * depth), bf16),
            ),
            in_specs=[pl.BlockSpec(memory_space=pl.ANY)] * 2,
            out_specs=(pl.BlockSpec(memory_space=pl.ANY),) * 5,
            scratch_shapes=[
                pltpu.VMEM((8, rows, 4 * depth), bf16),
                pltpu.VMEM((2, 4 * depth, C), bf16),
                pltpu.VMEM((2, 2, 2, 4, rows, W), f32),
                pltpu.VMEM((2, 2, 4, rows, W), f32),
                pltpu.VMEM((2, 2, 4, rows, W), f32),
                pltpu.VMEM((2, 2, 2, rows, W), f32),
                pltpu.VMEM((D3, 2, 2, rows, W), f32),
                pltpu.VMEM((D3, 2, rows, W), f32),
                pltpu.VMEM((2, 2, rows, W), bf16),
                pltpu.VMEM((DO, 2, 2, rows, W), bf16),
                dma((12, 2)), dma((12, 2)), dma((4,)),
                dma((tiles,)), dma((tiles,)), dma((paired,)), dma((paired,)),
                dma((16 + 2 * paired,)), dma((16 + 2 * paired,)), dma((2, 4)),
                dma((2, 2)), dma((2, 2)), dma((2, 2)), dma((2, 2)), dma((D3, 2)), dma((D3, 2)),
                dma((2, 2)), dma((DO, 2)), dma((DO, 2)), dma((paired, 2)),
                pltpu.SemaphoreType.REGULAR((3, 2)),
            ],
            compiler_params=pltpu.CompilerParams(
                collective_id=0, has_side_effects=True, vmem_limit_bytes=63 * 1024 * 1024),
            cost_estimate=pl.CostEstimate(
                flops=2 * 8 * rows * 2 * depth * columns, bytes_accessed=6 * depth * columns, transcendentals=0),
        )(a_rows, b_rows)
        return out[0]

    return jax.shard_map(local_block, mesh=mesh, in_specs=(spec_rows, spec_rows), out_specs=spec_rows, check_vma=False)
```

time: 2230 us -> 911 us (0.41)
  waiting for transfers between devices: 1710 us -> 0 us
  Pallas kernels: 0 us -> 904 us
  matrix products: 258 us -> 0 us
  blocking collectives: 192 us -> 0 us
  local copies, waits for them, and re-layouts: 43.3 us -> 6.9 us
    all_gather x1 -> x0, waiting for transfers between devices: 1100 us -> none  [local_block(): b_slab = lax.all_gather(b_rows, 'tp', axis=0, tiled=True)]
    pallas_call x0 -> x1, Pallas kernels: none -> 904 us  [local_block(): pl.pallas_call(kernel, name='matmul_reduce_scatter', out_shape=(jax.Shape...]
    reduce_scatter x1 -> x0, waiting for transfers between devices: 611 us -> none  [local_block(): summed = lax.psum_scatter(part_prod, 'dp', scatter_dimension=0, tiled=True)]
    dot_general x1 -> x0, matrix products: 258 us -> none  [local_block(): part_prod = jnp.dot(a_cols, b_slab, preferred_element_type=jnp.float32)]
    all_to_all x1 -> x0, blocking collectives: 192 us -> none  [local_block(): a_cols = lax.all_to_all(a_rows, 'dp', 1, 0, tiled=True)]
  transfers between devices with their start and end apart: 2 -> 0, of which waited for: 2 -> 0; matrix products, arithmetic and copies ran while one was open for 2% -> 0% of each run, Pallas kernels for 0% -> 0%
where the time goes in v3:
time: 911 us
  Pallas kernels  904 us (99%)
    pallas_call x1, Pallas kernels, local_block(): pl.pallas_call(kernel, name='matmul_reduce_scatter', out_shape=(jax.Shape...  904 us

profile of v3, /device:TPU:0, one launch (start us, length us, event | category | flops | bytes accessed | tf_op | source)
XLA Modules:
  0.0 910.9 jit_solution(2058116918092543159)
XLA Ops:
  0.0 904.0 %matmul_reduce_scatter.1 = (bf16[256,14336]{1,0:T(8,128)(2,1)}, bf16[42,2048,256]{2,1,0:T(8,128)(2,1)}, bf16[14,2048,256]{2,1,0:T(8,128)(2,1)}, bf16[14,2048,256]{2,1,0:T(8,128)(2,1)}, bf16[2,256,4096]{2,1,0:T(8,128)(2,1)}) custom-call(bf16[256,32768]{1,0:T(8,128)(2,1)} %a_hbm.1, bf16[2048,14336]{1,0:T(8,128)(2,1)} %b_hbm.1), custom_call_target="tpu_custom_call" | custom-call | flops 240518168576 | bytes 176160768 | tf_op jit(solution)/shard_map/matmul_reduce_scatter/pallas_call | solution.py:373
  904.0 6.9 copy.4
